TPU v7x, 128 devices: a whole 4x4x4 slice. The times are simulated.
128 devices in a mesh: row: 16 (over y, z), col: 8 (over x, core).
Axes of the slice: x: 4, y: 4, z: 4, core: 2. Of those that a mesh axis runs over, the one named last changes fastest.
Arguments:
- matrix_tiles: bfloat16 [16, 8, 96, 256, 256], P('row', 'col'), may hold values from -0.0546875 to 0.0546875
- tile_rows: int32 [16, 8, 96], P('row', 'col'), may hold values from 0 to 7, as said below
- tile_cols: int32 [16, 8, 96], P('row', 'col'), may hold values from 0 to 15
- tile_count: int32 [16, 8], P('row', 'col'), may hold values from 24 to 96, as said below
- x_start: float32 [32768, 256], P(('col', 'row')), may hold values from -5 to 5
- y_start: float32 [32768, 256], P(('row', 'col')), may hold values from 0 to 1
- cost_vector: float32 [32768, 256], P(('col', 'row')), may hold values from -6 to 6
- right_side: float32 [32768, 256], P(('row', 'col')), may hold values from -6 to 6
- lower_bound: float32 [32768, 256], P(('col', 'row')), may hold values from -1.5 to -0.3
- upper_bound: float32 [32768, 256], P(('col', 'row')), may hold values from 0.3 to 1.5
- step_primal: float32 [256], replicated, may hold values from 0.2 to 0.45
- step_dual: float32 [256], replicated, may hold values from 0.2 to 0.45
Outputs:
- primal_out: float32 [32768, 256], P(('col', 'row'))
- dual_out: float32 [32768, 256], P(('row', 'col'))
Inputs may be any that keep to these rules, and one draw needn't show every extreme that they name: Within one grid cell the pairs (tile_rows, tile_cols) of its slots are all different. `tile_count`: some grid cell has 96 used slots in every draw; slots at or above a cell's count are not part of A.
All inputs are finite; a program needn't handle non-finite values.
Results may differ from a plain program's by a relative error of at most 0.001.
Values may be sent and summed in bfloat16 or wider, within the bound.
No kernel may reach another device: no remote copies, remote signals or barrier semaphores. Data moves between devices by JAX's collectives and lax.ppermute only.
A program may use at most 128 MiB of HBM per device.

v0:
```python
import jax
import jax.numpy as jnp
from jax import lax
from jax.sharding import Mesh
from jax.sharding import PartitionSpec as P

NR_DEV = 8
SLOT_BLOCK = 16
ROW = ("row_0", "row_1")
COL = ("col_0", "col_1")
ROW_COL = ("row_0", "row_1", "col_0", "col_1")
COL_ROW = ("col_0", "col_1", "row_0", "row_1")
eps = 1e-06


def from_everyone(x, axis):
    devices = lax.axis_size(axis)
    return lax.all_to_all(jnp.broadcast_to(x[None], (devices, *x.shape)), axis, 0, 0, tiled=True)


def in_order(pieces, dim):
    dims = list(pieces.shape[1:])
    dims[dim] *= pieces.shape[0]
    return jnp.moveaxis(pieces, 0, dim).reshape(dims)


def gather_directly(x, axis, dim):
    pieces = from_everyone(x, axis)
    return in_order(pieces, dim)


def in_blocks(x, dim, devices):
    before, after = (x.shape[:dim], x.shape[dim + 1 :])
    return jnp.moveaxis(x.reshape(*before, devices, -1, *after), dim, 0)


def sum_at_owner(x, axis, dim):
    devices = lax.axis_size(axis)
    pieces = lax.all_to_all(in_blocks(x, dim, devices), axis, 0, 0, tiled=True)
    return jnp.sum(pieces, axis=0)


def one_axis_at_a_time(x, axes):
    for axis in axes:
        x = lax.psum(x, axis)
    return x


def forward_part(my_tiles, my_rows, my_cols, slot_count, segment):
    edge = my_tiles.shape[-1]
    batch_width = segment.shape[-1]
    x_tiles = segment.reshape(-1, edge, batch_width)
    slot_ids = jnp.arange(SLOT_BLOCK, dtype=jnp.int32)

    def forward_block_step(block_index, running):
        first_slot = block_index * SLOT_BLOCK
        tile_block = lax.dynamic_slice_in_dim(my_tiles, first_slot, SLOT_BLOCK, 0)
        row_block = lax.dynamic_slice_in_dim(my_rows, first_slot, SLOT_BLOCK, 0)
        col_block = lax.dynamic_slice_in_dim(my_cols, first_slot, SLOT_BLOCK, 0)
        in_use = first_slot + slot_ids < slot_count
        pieces = jnp.take(x_tiles, col_block, axis=0)
        products = jnp.einsum(
            "sij,sjb->sib", tile_block, pieces, preferred_element_type=jnp.float32
        )
        products = jnp.where(in_use[:, None, None], products, jnp.zeros_like(products))
        return running.at[row_block].add(products)

    blocks = (slot_count + SLOT_BLOCK - 1) // SLOT_BLOCK
    begin = jnp.zeros((NR_DEV, edge, batch_width), jnp.float32)
    return lax.fori_loop(0, blocks, forward_block_step, begin).reshape(-1, batch_width)


def backward_part(my_tiles, my_rows, my_cols, slot_count, segment, col_tiles):
    edge = my_tiles.shape[-1]
    batch_width = segment.shape[-1]
    y_tiles = segment.reshape(-1, edge, batch_width)
    slot_ids = jnp.arange(SLOT_BLOCK, dtype=jnp.int32)

    def backward_block_step(block_index, running):
        first_slot = block_index * SLOT_BLOCK
        tile_block = lax.dynamic_slice_in_dim(my_tiles, first_slot, SLOT_BLOCK, 0)
        row_block = lax.dynamic_slice_in_dim(my_rows, first_slot, SLOT_BLOCK, 0)
        col_block = lax.dynamic_slice_in_dim(my_cols, first_slot, SLOT_BLOCK, 0)
        in_use = first_slot + slot_ids < slot_count
        pieces = jnp.take(y_tiles, row_block, axis=0)
        products = jnp.einsum(
            "sij,sib->sjb", tile_block, pieces, preferred_element_type=jnp.float32
        )
        products = jnp.where(in_use[:, None, None], products, jnp.zeros_like(products))
        return running.at[col_block].add(products)

    blocks = (slot_count + SLOT_BLOCK - 1) // SLOT_BLOCK
    begin = jnp.zeros((col_tiles, edge, batch_width), jnp.float32)
    return lax.fori_loop(0, blocks, backward_block_step, begin).reshape(-1, batch_width)


def body(
    matrix_tiles,
    tile_rows,
    tile_cols,
    tile_count,
    x_start,
    y_start,
    cost_vector,
    right_side,
    lower_bound,
    upper_bound,
    step_primal,
    step_dual,
):
    my_tiles = matrix_tiles[0, 0]
    my_rows = tile_rows[0, 0]
    my_cols = tile_cols[0, 0]
    slot_count = tile_count[0, 0]
    row_devices = lax.axis_size(ROW)
    col_devices = lax.axis_size(COL)
    share = x_start.shape[0]
    edge = my_tiles.shape[-1]
    col_tiles = share * row_devices // edge
    total_cols = share * row_devices * col_devices
    total_rows = y_start.shape[0] * row_devices * col_devices

    def dual_rows(values):
        return gather_directly(values.astype(jnp.bfloat16), COL, 0)

    def row_sums(segment):
        return sum_at_owner(forward_part(my_tiles, my_rows, my_cols, slot_count, segment), COL, 0)

    x_base, cost_seg, lower_seg, upper_seg = (x_start, cost_vector, lower_bound, upper_bound)

    def column_sums(segment):
        partial_value = backward_part(my_tiles, my_rows, my_cols, slot_count, segment, col_tiles)
        return sum_at_owner(partial_value, ROW, 0)

    def spread(ahead):
        return gather_directly(ahead, ROW, 0)

    grad_zero = column_sums(dual_rows(y_start))
    primal_one = jnp.clip(x_base - step_primal * (cost_seg - grad_zero), lower_seg, upper_seg)
    primal_diff = primal_one - x_base
    move_primal = jnp.sum(primal_diff * primal_diff, axis=0)
    image_one = row_sums(spread((2.0 * primal_one - x_base).astype(jnp.bfloat16)))
    dual_one = jnp.maximum(y_start + step_dual * (right_side - image_one), 0.0)
    dual_diff = dual_one - y_start
    move_dual = jnp.sum(dual_diff * dual_diff, axis=0)
    move_primal, move_dual = (
        one_axis_at_a_time(move_primal, ROW_COL),
        one_axis_at_a_time(move_dual, ROW_COL),
    )
    weight = jnp.sqrt((move_dual / total_rows + eps) / (move_primal / total_cols + eps))
    grad_one = column_sums(dual_rows(dual_one))
    primal_two = jnp.clip(
        primal_one - step_primal / weight * (cost_seg - grad_one), lower_seg, upper_seg
    )
    image_two = row_sums(spread((2.0 * primal_two - primal_one).astype(jnp.bfloat16)))
    dual_out = jnp.maximum(dual_one + step_dual * weight * (right_side - image_two), 0.0)
    return (primal_two, dual_out)


def solution(mesh):
    torus = Mesh(mesh.devices.reshape(4, 4, 4, 2), ("row_0", "row_1", "col_0", "col_1"))
    in_specs = (
        P(ROW, COL, None, None, None),
        P(ROW, COL, None),
        P(ROW, COL, None),
        P(ROW, COL),
        P(COL_ROW, None),
        P(ROW_COL, None),
        P(COL_ROW, None),
        P(ROW_COL, None),
        P(COL_ROW, None),
        P(COL_ROW, None),
        P(),
        P(),
    )
    out_specs = (P(COL_ROW, None), P(ROW_COL, None))
    return jax.shard_map(body, mesh=torus, in_specs=in_specs, out_specs=out_specs, check_vma=False)
```

profile of v0, /device:TPU:16, one launch (start us, length us, event | category | flops | bytes accessed | tf_op | source)
XLA Modules:
  0.0 712.4 jit_solution(18077304454636752747)
XLA Ops:
  7.7 16.6 %copy.14 = bf16[96,256,256]{1,2,0:T(8,128)(2,1)} copy(bf16[96,256,256]{2,1,0:T(8,128)(2,1)} %bitcast.5) | data formatting | bytes 25165824
  26.7 92.7 %while.44 = (s32[]{:T(128)}, f32[16,256,256]{2,1,0:T(8,128)}, s32[]{:T(128)}, s32[96]{0:T(128)S(1)}, s32[]{:T(128)}, /*index=5*/bf16[96,256,256]{1,2,0:T(8,128)(...) while((s32[]{:T(128)}, f32[16,256,256]{2,1,0:T(8,128)}, ...), condition=%wide.region_2.4_spmd.clone, body=%wide.region_0.3_spmd.clone.sunk | while | flops 540017856 | bytes 25170616 | solution.py:94
  28.1 4.3 convolution_select_fusion.8
  32.5 9.5 %scatter_fusion = f32[16,256,256]{2,1,0:T(8,128)} fusion(f32[16,256,256]{2,1,0:T(8,128)} %get-tuple-element.621, s32[16]{0:T(128)S(1)} %compare_select_fusion.16, f32[16,256,256]{2,1,0:T(8,128)} %convolution_select_fusion.8), kind=kCustom, calls=%fused_computation.4.clone.clone.1 | custom fusion | flops 1048576 | bytes 12582976 | tf_op jit(solution)/shard_map/while/body/scatter-add | solution.py:90
  43.5 4.3 convolution_select_fusion.8
  47.9 9.6 %scatter_fusion = f32[16,256,256]{2,1,0:T(8,128)} fusion(f32[16,256,256]{2,1,0:T(8,128)} %get-tuple-element.621, s32[16]{0:T(128)S(1)} %compare_select_fusion.16, f32[16,256,256]{2,1,0:T(8,128)} %convolution_select_fusion.8), kind=kCustom, calls=%fused_computation.4.clone.clone.1 | custom fusion | flops 1048576 | bytes 12582976 | tf_op jit(solution)/shard_map/while/body/scatter-add | solution.py:90
  58.9 4.3 convolution_select_fusion.8
  63.3 9.7 %scatter_fusion = f32[16,256,256]{2,1,0:T(8,128)} fusion(f32[16,256,256]{2,1,0:T(8,128)} %get-tuple-element.621, s32[16]{0:T(128)S(1)} %compare_select_fusion.16, f32[16,256,256]{2,1,0:T(8,128)} %convolution_select_fusion.8), kind=kCustom, calls=%fused_computation.4.clone.clone.1 | custom fusion | flops 1048576 | bytes 12582976 | tf_op jit(solution)/shard_map/while/body/scatter-add | solution.py:90
  74.5 4.3 convolution_select_fusion.8
  78.9 9.6 %scatter_fusion = f32[16,256,256]{2,1,0:T(8,128)} fusion(f32[16,256,256]{2,1,0:T(8,128)} %get-tuple-element.621, s32[16]{0:T(128)S(1)} %compare_select_fusion.16, f32[16,256,256]{2,1,0:T(8,128)} %convolution_select_fusion.8), kind=kCustom, calls=%fused_computation.4.clone.clone.1 | custom fusion | flops 1048576 | bytes 12582976 | tf_op jit(solution)/shard_map/while/body/scatter-add | solution.py:90
  89.9 4.3 convolution_select_fusion.8
  94.4 9.8 %scatter_fusion = f32[16,256,256]{2,1,0:T(8,128)} fusion(f32[16,256,256]{2,1,0:T(8,128)} %get-tuple-element.621, s32[16]{0:T(128)S(1)} %compare_select_fusion.16, f32[16,256,256]{2,1,0:T(8,128)} %convolution_select_fusion.8), kind=kCustom, calls=%fused_computation.4.clone.clone.1 | custom fusion | flops 1048576 | bytes 12582976 | tf_op jit(solution)/shard_map/while/body/scatter-add | solution.py:90
  105.5 4.3 convolution_select_fusion.8
  110.0 9.4 %scatter_fusion = f32[16,256,256]{2,1,0:T(8,128)} fusion(f32[16,256,256]{2,1,0:T(8,128)} %get-tuple-element.621, s32[16]{0:T(128)S(1)} %compare_select_fusion.16, f32[16,256,256]{2,1,0:T(8,128)} %convolution_select_fusion.8), kind=kCustom, calls=%fused_computation.4.clone.clone.1 | custom fusion | flops 1048576 | bytes 12582976 | tf_op jit(solution)/shard_map/while/body/scatter-add | solution.py:90
  119.4 55.2 %all_to_all.40 = f32[16,256,256]{2,1,0:T(8,128)} all-to-all(f32[16,256,256]{2,1,0:T(8,128)} %get-tuple-element.196), channel_id=1, replica_groups=mesh['row_0'=4,'row_1'=4,'col_0'=4,'col_1'=2] {'row_0','row_1'}, dimensions={0} | all-to-all | bytes 8388608 | tf_op jit(solution)/shard_map/all_to_all | solution.py:39
  179.5 6.7 all-to-all-start.2
  186.2 25.3 %all-to-all-done.2 = bf16[16,256,256]{2,1,0:T(8,128)(2,1)} async-done(((bf16[16,256,256]{2,1,0:T(8,128)(2,1)}), bf16[16,256,256]{2,1,0:T(8,128)(2,1)}, u32[]{:S(2)}, u32[]{:S(2)}) %all-to-all-start.2) | async-done | bytes 2097184 | tf_op jit(solution)/shard_map/all_to_all | solution.py:18
  211.7 93.2 %while.45 = (s32[]{:T(128)}, f32[8,256,256]{2,1,0:T(8,128)S(1)}, s32[]{:T(128)}, s32[96]{0:T(128)S(1)}, s32[]{:T(128)}, /*index=5*/bf16[96,256,256]{2,1,0:T(8,12...) while((s32[]{:T(128)}, f32[8,256,256]{2,1,0:T(8,128)S(1)}, ...), condition=%wide.region_6.9_spmd.clone, body=%wide.region_4.8_spmd.clone.sunk | while | flops 540017856 | bytes 25170616 | solution.py:70
  216.0 5.0 convolution_select_fusion.9
  221.1 6.2 scatter_fusion.1
  231.6 5.0 convolution_select_fusion.9
  236.6 6.1 scatter_fusion.1
  247.1 5.0 convolution_select_fusion.9
  252.1 6.2 scatter_fusion.1
  262.6 5.0 convolution_select_fusion.9
  267.7 6.1 scatter_fusion.1
  278.1 5.0 convolution_select_fusion.9
  283.2 6.2 scatter_fusion.1
  293.7 5.0 convolution_select_fusion.9
  298.7 6.1 scatter_fusion.1
  304.9 34.1 %all_to_all.41 = f32[8,256,256]{2,1,0:T(8,128)} all-to-all(f32[8,256,256]{2,1,0:T(8,128)S(1)} %get-tuple-element.197), channel_id=1, replica_groups=mesh['row_0'=4,'row_1'=4,'col_0'=4,'col_1'=2] {'col_0','col_1'}, dimensions={0} | all-to-all | bytes 4194304 | tf_op jit(solution)/shard_map/all_to_all | solution.py:39
  345.6 15.9 %all-to-all-done.4 = bf16[8,256,256]{2,1,0:T(8,128)(2,1)S(1)} async-done(((bf16[8,256,256]{2,1,0:T(8,128)(2,1)}), bf16[8,256,256]{2,1,0:T(8,128)(2,1)S(1)}, u32[]{:S(2)}, u32[]{:S(2)}) %all-to-all-start.4) | async-done | bytes 1048608 | tf_op jit(solution)/shard_map/all_to_all | solution.py:18
  363.9 92.7 %while.46 = (s32[]{:T(128)}, f32[16,256,256]{2,1,0:T(8,128)}, s32[]{:T(128)}, s32[96]{0:T(128)S(1)}, s32[]{:T(128)}, /*index=5*/bf16[96,256,256]{1,2,0:T(8,128)(...) while((s32[]{:T(128)}, f32[16,256,256]{2,1,0:T(8,128)}, ...), condition=%wide.region_20.23_spmd.clone, body=%wide.region_18.22_spmd.clone.sunk | while | flops 540017856 | bytes 25170616 | solution.py:94
  365.3 4.3 convolution_select_fusion.10
  369.7 9.5 %scatter_fusion.2 = f32[16,256,256]{2,1,0:T(8,128)} fusion(f32[16,256,256]{2,1,0:T(8,128)} %get-tuple-element.693, s32[16]{0:T(128)S(1)} %compare_select_fusion.18, f32[16,256,256]{2,1,0:T(8,128)} %convolution_select_fusion.10), kind=kCustom, calls=%fused_computation.6.clone.clone.1 | custom fusion | flops 1048576 | bytes 12582976 | tf_op jit(solution)/shard_map/while/body/scatter-add | solution.py:90
  380.6 4.3 convolution_select_fusion.10
  385.1 9.6 %scatter_fusion.2 = f32[16,256,256]{2,1,0:T(8,128)} fusion(f32[16,256,256]{2,1,0:T(8,128)} %get-tuple-element.693, s32[16]{0:T(128)S(1)} %compare_select_fusion.18, f32[16,256,256]{2,1,0:T(8,128)} %convolution_select_fusion.10), kind=kCustom, calls=%fused_computation.6.clone.clone.1 | custom fusion | flops 1048576 | bytes 12582976 | tf_op jit(solution)/shard_map/while/body/scatter-add | solution.py:90
  396.0 4.3 convolution_select_fusion.10
  400.5 9.7 %scatter_fusion.2 = f32[16,256,256]{2,1,0:T(8,128)} fusion(f32[16,256,256]{2,1,0:T(8,128)} %get-tuple-element.693, s32[16]{0:T(128)S(1)} %compare_select_fusion.18, f32[16,256,256]{2,1,0:T(8,128)} %convolution_select_fusion.10), kind=kCustom, calls=%fused_computation.6.clone.clone.1 | custom fusion | flops 1048576 | bytes 12582976 | tf_op jit(solution)/shard_map/while/body/scatter-add | solution.py:90
  411.6 4.3 convolution_select_fusion.10
  416.0 9.6 %scatter_fusion.2 = f32[16,256,256]{2,1,0:T(8,128)} fusion(f32[16,256,256]{2,1,0:T(8,128)} %get-tuple-element.693, s32[16]{0:T(128)S(1)} %compare_select_fusion.18, f32[16,256,256]{2,1,0:T(8,128)} %convolution_select_fusion.10), kind=kCustom, calls=%fused_computation.6.clone.clone.1 | custom fusion | flops 1048576 | bytes 12582976 | tf_op jit(solution)/shard_map/while/body/scatter-add | solution.py:90
  431.5 9.8 %scatter_fusion.2 = f32[16,256,256]{2,1,0:T(8,128)} fusion(f32[16,256,256]{2,1,0:T(8,128)} %get-tuple-element.693, s32[16]{0:T(128)S(1)} %compare_select_fusion.18, f32[16,256,256]{2,1,0:T(8,128)} %convolution_select_fusion.10), kind=kCustom, calls=%fused_computation.6.clone.clone.1 | custom fusion | flops 1048576 | bytes 12582976 | tf_op jit(solution)/shard_map/while/body/scatter-add | solution.py:90
  442.7 4.3 convolution_select_fusion.10
  447.1 9.4 %scatter_fusion.2 = f32[16,256,256]{2,1,0:T(8,128)} fusion(f32[16,256,256]{2,1,0:T(8,128)} %get-tuple-element.693, s32[16]{0:T(128)S(1)} %compare_select_fusion.18, f32[16,256,256]{2,1,0:T(8,128)} %convolution_select_fusion.10), kind=kCustom, calls=%fused_computation.6.clone.clone.1 | custom fusion | flops 1048576 | bytes 12582976 | tf_op jit(solution)/shard_map/while/body/scatter-add | solution.py:90
  456.5 7.4 %all-to-all-start.5 = ((f32[16,256,256]{2,1,0:T(8,128)}), f32[16,256,256]{2,1,0:T(8,128)}, u32[]{:S(2)}, u32[]{:S(2)}) async-start(f32[16,256,256]{2,1,0:T(8,128)} %get-tuple-element.198), calls=%async_computation.5 | async-start | bytes 8388608 | tf_op jit(solution)/shard_map/all_to_all | solution.py:39
  463.9 51.3 %all-reduce.2 = (f32[256]{0:T(256)S(1)}, f32[256]{0:T(256)S(1)}) all-reduce(f32[256]{0:T(256)S(1)} %get-tuple-element.378, f32[256]{0:T(256)S(1)} %get-tuple-element.376), channel_id=1, replica_groups=mesh['row_0'=4,'row_1'=4,'col_0'=4,'col_1'=2] {'row_0'}, use_global_device_ids=true, to_apply=%region_14.17 | all-reduce | flops 512 | bytes 4096 | tf_op jit(solution)/shard_map/psum | solution.py:45
  515.3 9.3 %all-reduce.1 = (f32[256]{0:T(256)S(1)}, f32[256]{0:T(256)S(1)}) all-reduce(f32[256]{0:T(256)S(1)} %get-tuple-element.360, f32[256]{0:T(256)S(1)} %get-tuple-element.361), channel_id=1, replica_groups=mesh['row_0'=4,'row_1'=4,'col_0'=4,'col_1'=2] {'row_1'}, use_global_device_ids=true, to_apply=%region_15.18 | all-reduce | flops 512 | bytes 4096 | tf_op jit(solution)/shard_map/psum | solution.py:45
  524.6 19.5 %all-reduce = (f32[256]{0:T(256)S(1)}, f32[256]{0:T(256)S(1)}) all-reduce(f32[256]{0:T(256)S(1)} %get-tuple-element.358, f32[256]{0:T(256)S(1)} %get-tuple-element.359), channel_id=1, replica_groups=mesh['row_0'=4,'row_1'=4,'col_0'=4,'col_1'=2] {'col_0'}, use_global_device_ids=true, to_apply=%region_16.19 | all-reduce | flops 512 | bytes 4096 | tf_op jit(solution)/shard_map/psum | solution.py:45
  551.6 5.9 all-to-all-start.6
  557.5 28.2 %all-to-all-done.6 = bf16[16,256,256]{2,1,0:T(8,128)(2,1)} async-done(((bf16[16,256,256]{2,1,0:T(8,128)(2,1)}), bf16[16,256,256]{2,1,0:T(8,128)(2,1)}, u32[]{:S(2)}, u32[]{:S(2)}) %all-to-all-start.6) | async-done | bytes 2097184 | tf_op jit(solution)/shard_map/all_to_all | solution.py:18
  585.9 93.5 %while.47 = (s32[]{:T(128)}, f32[8,256,256]{2,1,0:T(8,128)S(1)}, s32[]{:T(128)}, s32[96]{0:T(128)S(1)}, s32[]{:T(128)}, /*index=5*/bf16[96,256,256]{2,1,0:T(8,12...) while((s32[]{:T(128)}, f32[8,256,256]{2,1,0:T(8,128)S(1)}, ...), condition=%wide.region_24.27_spmd.clone, body=%wide.region_22.26_spmd.clone.sunk | while | flops 540017856 | bytes 25170616 | solution.py:70
  590.5 5.0 convolution_select_fusion.11
  595.5 6.2 scatter_fusion.3
  606.0 5.0 convolution_select_fusion.11
  611.1 6.1 scatter_fusion.3
  621.6 5.0 convolution_select_fusion.11
  626.6 6.2 scatter_fusion.3
  637.2 5.0 convolution_select_fusion.11
  642.2 6.1 scatter_fusion.3
  652.7 5.0 convolution_select_fusion.11
  657.7 6.2 scatter_fusion.3
  668.3 5.0 convolution_select_fusion.11
  673.3 6.1 scatter_fusion.3
  679.5 30.4 %all_to_all.42 = f32[8,256,256]{2,1,0:T(8,128)} all-to-all(f32[8,256,256]{2,1,0:T(8,128)S(1)} %get-tuple-element.199), channel_id=1, replica_groups=mesh['row_0'=4,'row_1'=4,'col_0'=4,'col_1'=2] {'col_0','col_1'}, dimensions={0} | all-to-all | bytes 4194304 | tf_op jit(solution)/shard_map/all_to_all | solution.py:39
  (155 shorter events, 107.9 us)
Async XLA Ops:
  2.7 21.6 %all-to-all-start = ((bf16[8,256,256]{2,1,0:T(8,128)(2,1)}), bf16[8,256,256]{2,1,0:T(8,128)(2,1)S(1)}, u32[]{:S(2)}, u32[]{:S(2)}) async-start(bf16[8,256,256]{2,1,0:T(8,128)(2,1)} %broadcast_in_dim.85), calls=%async_computation | async-start | bytes 2097152 | tf_op jit(solution)/shard_map/all_to_all | solution.py:18
  24.3 2.4 copy-start.12
  24.3 2.4 copy-start.13
  174.5 2.6 copy-start.4
  174.5 2.6 copy-start.6
  174.5 2.6 copy-start.8
  174.5 2.6 copy-start.10
  174.5 2.6 copy-start.14
  177.3 0.7 copy-start
  179.5 32.0 %all-to-all-start.2 = ((bf16[16,256,256]{2,1,0:T(8,128)(2,1)}), bf16[16,256,256]{2,1,0:T(8,128)(2,1)}, u32[]{:S(2)}, u32[]{:S(2)}) async-start(bf16[16,256,256]{2,1,0:T(8,128)(2,1)} %broadcast_in_dim.86), calls=%async_computation.2 | async-start | bytes 4194304 | tf_op jit(solution)/shard_map/all_to_all | solution.py:18
  339.0 1.8 copy-start.2
  339.0 1.8 copy-start.5
  339.0 1.8 copy-start.15
  342.1 19.4 %all-to-all-start.4 = ((bf16[8,256,256]{2,1,0:T(8,128)(2,1)}), bf16[8,256,256]{2,1,0:T(8,128)(2,1)S(1)}, u32[]{:S(2)}, u32[]{:S(2)}) async-start(bf16[8,256,256]{2,1,0:T(8,128)(2,1)} %broadcast_in_dim.87), calls=%async_computation.4 | async-start | bytes 2097152 | tf_op jit(solution)/shard_map/all_to_all | solution.py:18
  456.5 90.1 %all-to-all-start.5 = ((f32[16,256,256]{2,1,0:T(8,128)}), f32[16,256,256]{2,1,0:T(8,128)}, u32[]{:S(2)}, u32[]{:S(2)}) async-start(f32[16,256,256]{2,1,0:T(8,128)} %get-tuple-element.198), calls=%async_computation.5 | async-start | bytes 8388608 | tf_op jit(solution)/shard_map/all_to_all | solution.py:39
  546.6 2.6 copy-start.1
  546.6 2.6 copy-start.7
  546.6 2.6 copy-start.9
  546.6 2.6 copy-start.11
  551.6 34.1 %all-to-all-start.6 = ((bf16[16,256,256]{2,1,0:T(8,128)(2,1)}), bf16[16,256,256]{2,1,0:T(8,128)(2,1)}, u32[]{:S(2)}, u32[]{:S(2)}) async-start(bf16[16,256,256]{2,1,0:T(8,128)(2,1)} %broadcast_in_dim.88), calls=%async_computation.6 | async-start | bytes 4194304 | tf_op jit(solution)/shard_map/all_to_all | solution.py:18
  709.8 1.8 copy-start.3
where the time goes:
time: 716 us; the launch traced here: 712 us
  other arithmetic  220 us (31%)
  blocking collectives  202 us (28%)
  matrix products  112 us (16%)
  local copies, waits for them, and re-layouts  79.1 us (11%)
  waiting for transfers between devices  69.3 us (10%)
  starting transfers between devices  27.9 us (4%)
    all_to_all x3, blocking collectives, sum_at_owner(): pieces = lax.all_to_all(in_blocks(x, dim, devices), axis, 0, 0, tiled=True)  120 us
    scatter-add x12, other arithmetic, backward_block_step(): return running.at[col_block].add(products)  115 us
    psum x4, blocking collectives, one_axis_at_a_time(): x = lax.psum(x, axis)  82.6 us
    scatter-add x12, other arithmetic, forward_block_step(): return running.at[row_block].add(products)  73.8 us
    all_to_all x4, waiting for transfers between devices, from_everyone(): lax.all_to_all(jnp.broadcast_to(x[None], (devices, *x.shape)), axis, 0, 0...  69.3 us
    dot_general x12, matrix products, forward_block_step(): jnp.einsum('sij,sjb->sib', tile_block, pieces, preferred_element_type=jnp...  59.5 us
    dot_general x12, matrix products, backward_block_step(): jnp.einsum('sij,sib->sjb', tile_block, pieces, preferred_element_type=jnp...  52.1 us
    gather x12, local copies, waits for them, and re-layouts, forward_block_step(): pieces = jnp.take(x_tiles, col_block, axis=0)  43.1 us
  transfers between devices with their start and end apart: 5, of which 3 were waited for; matrix products, arithmetic and copies ran while one was open for 2% of the time, Pallas kernels for 0%

commit v1 on v0

--- a/solution.py
+++ b/solution.py
@@ -42,7 +42,8 @@
 
 def one_axis_at_a_time(x, axes):
     for axis in axes:
-        x = lax.psum(x, axis)
+        parts = lax.all_gather(x, axis, axis=0, tiled=False)
+        x = parts.sum(axis=0)
     return x
 
 

time: 716 us -> 740 us (1.034)
  blocking collectives: 202 us -> 224 us
    all_gather x0 -> x8, blocking collectives: none -> 105 us  [one_axis_at_a_time(): parts = lax.all_gather(x, axis, axis=0, tiled=False)]
    psum x4 -> x0, blocking collectives: 82.6 us -> none  [one_axis_at_a_time(): x = lax.psum(x, axis)]
where the time goes in v1:
time: 740 us; the launch traced here: 737 us
  blocking collectives  224 us (30%)
  other arithmetic  220 us (30%)
  matrix products  112 us (15%)
  local copies, waits for them, and re-layouts  79.1 us (11%)
  waiting for transfers between devices  70.2 us (9%)
  starting transfers between devices  29.3 us (4%)
    all_to_all x3, blocking collectives, sum_at_owner(): pieces = lax.all_to_all(in_blocks(x, dim, devices), axis, 0, 0, tiled=True)  119 us
    scatter-add x12, other arithmetic, backward_block_step(): return running.at[col_block].add(products)  115 us
    all_gather x8, blocking collectives, one_axis_at_a_time(): parts = lax.all_gather(x, axis, axis=0, tiled=False)  105 us
    scatter-add x12, other arithmetic, forward_block_step(): return running.at[row_block].add(products)  73.8 us
    all_to_all x4, waiting for transfers between devices, from_everyone(): lax.all_to_all(jnp.broadcast_to(x[None], (devices, *x.shape)), axis, 0, 0...  70.2 us
    dot_general x12, matrix products, forward_block_step(): jnp.einsum('sij,sjb->sib', tile_block, pieces, preferred_element_type=jnp...  59.5 us
    dot_general x12, matrix products, backward_block_step(): jnp.einsum('sij,sib->sjb', tile_block, pieces, preferred_element_type=jnp...  52.2 us
    gather x12, local copies, waits for them, and re-layouts, forward_block_step(): pieces = jnp.take(x_tiles, col_block, axis=0)  43.1 us
  transfers between devices with their start and end apart: 5, of which 3 were waited for; matrix products, arithmetic and copies ran while one was open for 2% of the time, Pallas kernels for 0%

profile of v1, /device:TPU:16, one launch (start us, length us, event | category | flops | bytes accessed | tf_op | source)
XLA Modules:
  0.0 736.6 jit_solution(14156793891613409779)
XLA Ops:
  7.7 16.6 %copy.16 = bf16[96,256,256]{1,2,0:T(8,128)(2,1)} copy(bf16[96,256,256]{2,1,0:T(8,128)(2,1)} %bitcast.13) | data formatting | bytes 25165824
  26.7 92.6 %while.44 = (s32[]{:T(128)}, f32[16,256,256]{2,1,0:T(8,128)}, s32[]{:T(128)}, s32[96]{0:T(128)S(1)}, s32[]{:T(128)}, /*index=5*/bf16[96,256,256]{1,2,0:T(8,128)(...) while((s32[]{:T(128)}, f32[16,256,256]{2,1,0:T(8,128)}, ...), condition=%wide.region_2.4_spmd.clone, body=%wide.region_0.3_spmd.clone.sunk | while | flops 540017856 | bytes 25170616 | solution.py:95
  28.1 4.4 convolution_select_fusion.8
  32.5 9.5 %scatter_fusion = f32[16,256,256]{2,1,0:T(8,128)} fusion(f32[16,256,256]{2,1,0:T(8,128)} %get-tuple-element.629, s32[16]{0:T(128)S(1)} %compare_select_fusion.16, f32[16,256,256]{2,1,0:T(8,128)} %convolution_select_fusion.8), kind=kCustom, calls=%fused_computation.4.clone.clone.1 | custom fusion | flops 1048576 | bytes 12582976 | tf_op jit(solution)/shard_map/while/body/scatter-add | solution.py:91
  47.9 9.5 %scatter_fusion = f32[16,256,256]{2,1,0:T(8,128)} fusion(f32[16,256,256]{2,1,0:T(8,128)} %get-tuple-element.629, s32[16]{0:T(128)S(1)} %compare_select_fusion.16, f32[16,256,256]{2,1,0:T(8,128)} %convolution_select_fusion.8), kind=kCustom, calls=%fused_computation.4.clone.clone.1 | custom fusion | flops 1048576 | bytes 12582976 | tf_op jit(solution)/shard_map/while/body/scatter-add | solution.py:91
  58.8 4.4 convolution_select_fusion.8
  63.3 9.7 %scatter_fusion = f32[16,256,256]{2,1,0:T(8,128)} fusion(f32[16,256,256]{2,1,0:T(8,128)} %get-tuple-element.629, s32[16]{0:T(128)S(1)} %compare_select_fusion.16, f32[16,256,256]{2,1,0:T(8,128)} %convolution_select_fusion.8), kind=kCustom, calls=%fused_computation.4.clone.clone.1 | custom fusion | flops 1048576 | bytes 12582976 | tf_op jit(solution)/shard_map/while/body/scatter-add | solution.py:91
  74.4 4.4 convolution_select_fusion.8
  78.9 9.6 %scatter_fusion = f32[16,256,256]{2,1,0:T(8,128)} fusion(f32[16,256,256]{2,1,0:T(8,128)} %get-tuple-element.629, s32[16]{0:T(128)S(1)} %compare_select_fusion.16, f32[16,256,256]{2,1,0:T(8,128)} %convolution_select_fusion.8), kind=kCustom, calls=%fused_computation.4.clone.clone.1 | custom fusion | flops 1048576 | bytes 12582976 | tf_op jit(solution)/shard_map/while/body/scatter-add | solution.py:91
  89.9 4.4 convolution_select_fusion.8
  94.3 9.7 %scatter_fusion = f32[16,256,256]{2,1,0:T(8,128)} fusion(f32[16,256,256]{2,1,0:T(8,128)} %get-tuple-element.629, s32[16]{0:T(128)S(1)} %compare_select_fusion.16, f32[16,256,256]{2,1,0:T(8,128)} %convolution_select_fusion.8), kind=kCustom, calls=%fused_computation.4.clone.clone.1 | custom fusion | flops 1048576 | bytes 12582976 | tf_op jit(solution)/shard_map/while/body/scatter-add | solution.py:91
  105.5 4.3 convolution_select_fusion.8
  109.9 9.4 %scatter_fusion = f32[16,256,256]{2,1,0:T(8,128)} fusion(f32[16,256,256]{2,1,0:T(8,128)} %get-tuple-element.629, s32[16]{0:T(128)S(1)} %compare_select_fusion.16, f32[16,256,256]{2,1,0:T(8,128)} %convolution_select_fusion.8), kind=kCustom, calls=%fused_computation.4.clone.clone.1 | custom fusion | flops 1048576 | bytes 12582976 | tf_op jit(solution)/shard_map/while/body/scatter-add | solution.py:91
  119.3 55.2 %all_to_all.40 = f32[16,256,256]{2,1,0:T(8,128)} all-to-all(f32[16,256,256]{2,1,0:T(8,128)} %get-tuple-element.196), channel_id=1, replica_groups=mesh['row_0'=4,'row_1'=4,'col_0'=4,'col_1'=2] {'row_0','row_1'}, dimensions={0} | all-to-all | bytes 8388608 | tf_op jit(solution)/shard_map/all_to_all | solution.py:39
  179.5 6.7 all-to-all-start.2
  186.2 25.4 %all-to-all-done.2 = bf16[16,256,256]{2,1,0:T(8,128)(2,1)} async-done(((bf16[16,256,256]{2,1,0:T(8,128)(2,1)}), bf16[16,256,256]{2,1,0:T(8,128)(2,1)}, u32[]{:S(2)}, u32[]{:S(2)}) %all-to-all-start.2) | async-done | bytes 2097184 | tf_op jit(solution)/shard_map/all_to_all | solution.py:18
  211.7 93.2 %while.45 = (s32[]{:T(128)}, f32[8,256,256]{2,1,0:T(8,128)S(1)}, s32[]{:T(128)}, s32[96]{0:T(128)S(1)}, s32[]{:T(128)}, /*index=5*/bf16[96,256,256]{2,1,0:T(8,12...) while((s32[]{:T(128)}, f32[8,256,256]{2,1,0:T(8,128)S(1)}, ...), condition=%wide.region_6.9_spmd.clone, body=%wide.region_4.8_spmd.clone.sunk | while | flops 540017856 | bytes 25170616 | solution.py:71
  216.1 5.0 convolution_select_fusion.9
  221.1 6.2 scatter_fusion.1
  231.6 5.0 convolution_select_fusion.9
  236.7 6.1 scatter_fusion.1
  247.1 5.0 convolution_select_fusion.9
  252.2 6.2 scatter_fusion.1
  262.7 5.0 convolution_select_fusion.9
  267.7 6.1 scatter_fusion.1
  278.2 5.0 convolution_select_fusion.9
  283.2 6.2 scatter_fusion.1
  293.7 5.0 convolution_select_fusion.9
  298.8 6.1 scatter_fusion.1
  304.9 33.5 %all_to_all.41 = f32[8,256,256]{2,1,0:T(8,128)} all-to-all(f32[8,256,256]{2,1,0:T(8,128)S(1)} %get-tuple-element.197), channel_id=1, replica_groups=mesh['row_0'=4,'row_1'=4,'col_0'=4,'col_1'=2] {'col_0','col_1'}, dimensions={0} | all-to-all | bytes 4194304 | tf_op jit(solution)/shard_map/all_to_all | solution.py:39
  345.1 15.9 %all-to-all-done.4 = bf16[8,256,256]{2,1,0:T(8,128)(2,1)S(1)} async-done(((bf16[8,256,256]{2,1,0:T(8,128)(2,1)}), bf16[8,256,256]{2,1,0:T(8,128)(2,1)S(1)}, u32[]{:S(2)}, u32[]{:S(2)}) %all-to-all-start.4) | async-done | bytes 1048608 | tf_op jit(solution)/shard_map/all_to_all | solution.py:18
  363.3 92.6 %while.46 = (s32[]{:T(128)}, f32[16,256,256]{2,1,0:T(8,128)}, s32[]{:T(128)}, s32[96]{0:T(128)S(1)}, s32[]{:T(128)}, /*index=5*/bf16[96,256,256]{1,2,0:T(8,128)(...) while((s32[]{:T(128)}, f32[16,256,256]{2,1,0:T(8,128)}, ...), condition=%wide.region_20.23_spmd.clone, body=%wide.region_18.22_spmd.clone.sunk | while | flops 540017856 | bytes 25170616 | solution.py:95
  369.1 9.5 %scatter_fusion.2 = f32[16,256,256]{2,1,0:T(8,128)} fusion(f32[16,256,256]{2,1,0:T(8,128)} %get-tuple-element.701, s32[16]{0:T(128)S(1)} %compare_select_fusion.18, f32[16,256,256]{2,1,0:T(8,128)} %convolution_select_fusion.10), kind=kCustom, calls=%fused_computation.6.clone.clone.1 | custom fusion | flops 1048576 | bytes 12582976 | tf_op jit(solution)/shard_map/while/body/scatter-add | solution.py:91
  384.5 9.5 %scatter_fusion.2 = f32[16,256,256]{2,1,0:T(8,128)} fusion(f32[16,256,256]{2,1,0:T(8,128)} %get-tuple-element.701, s32[16]{0:T(128)S(1)} %compare_select_fusion.18, f32[16,256,256]{2,1,0:T(8,128)} %convolution_select_fusion.10), kind=kCustom, calls=%fused_computation.6.clone.clone.1 | custom fusion | flops 1048576 | bytes 12582976 | tf_op jit(solution)/shard_map/while/body/scatter-add | solution.py:91
  395.5 4.4 convolution_select_fusion.10
  399.9 9.7 %scatter_fusion.2 = f32[16,256,256]{2,1,0:T(8,128)} fusion(f32[16,256,256]{2,1,0:T(8,128)} %get-tuple-element.701, s32[16]{0:T(128)S(1)} %compare_select_fusion.18, f32[16,256,256]{2,1,0:T(8,128)} %convolution_select_fusion.10), kind=kCustom, calls=%fused_computation.6.clone.clone.1 | custom fusion | flops 1048576 | bytes 12582976 | tf_op jit(solution)/shard_map/while/body/scatter-add | solution.py:91
  411.0 4.4 convolution_select_fusion.10
  415.5 9.6 %scatter_fusion.2 = f32[16,256,256]{2,1,0:T(8,128)} fusion(f32[16,256,256]{2,1,0:T(8,128)} %get-tuple-element.701, s32[16]{0:T(128)S(1)} %compare_select_fusion.18, f32[16,256,256]{2,1,0:T(8,128)} %convolution_select_fusion.10), kind=kCustom, calls=%fused_computation.6.clone.clone.1 | custom fusion | flops 1048576 | bytes 12582976 | tf_op jit(solution)/shard_map/while/body/scatter-add | solution.py:91
  426.5 4.4 convolution_select_fusion.10
  431.0 9.7 %scatter_fusion.2 = f32[16,256,256]{2,1,0:T(8,128)} fusion(f32[16,256,256]{2,1,0:T(8,128)} %get-tuple-element.701, s32[16]{0:T(128)S(1)} %compare_select_fusion.18, f32[16,256,256]{2,1,0:T(8,128)} %convolution_select_fusion.10), kind=kCustom, calls=%fused_computation.6.clone.clone.1 | custom fusion | flops 1048576 | bytes 12582976 | tf_op jit(solution)/shard_map/while/body/scatter-add | solution.py:91
  446.5 9.4 %scatter_fusion.2 = f32[16,256,256]{2,1,0:T(8,128)} fusion(f32[16,256,256]{2,1,0:T(8,128)} %get-tuple-element.701, s32[16]{0:T(128)S(1)} %compare_select_fusion.18, f32[16,256,256]{2,1,0:T(8,128)} %convolution_select_fusion.10), kind=kCustom, calls=%fused_computation.6.clone.clone.1 | custom fusion | flops 1048576 | bytes 12582976 | tf_op jit(solution)/shard_map/while/body/scatter-add | solution.py:91
  455.9 8.0 %all-to-all-start.5 = ((f32[16,256,256]{2,1,0:T(8,128)}), f32[16,256,256]{2,1,0:T(8,128)}, u32[]{:S(2)}, u32[]{:S(2)}) async-start(f32[16,256,256]{2,1,0:T(8,128)} %get-tuple-element.198), calls=%async_computation.5 | async-start | bytes 8388608 | tf_op jit(solution)/shard_map/all_to_all | solution.py:39
  463.9 50.9 %all-gather.12 = f32[4,1,256]{2,1,0:T(1,128)S(1)} all-gather(f32[1,1,256]{2,1,0:T(1,128)S(1)} %bitcast.17), channel_id=6, replica_groups=mesh['row_0'=4,'row_1'=4,'col_0'=4,'col_1'=2] {'row_0'}, dimensions={0}, use_global_device_ids=true | all-gather | bytes 5120 | tf_op jit(solution)/shard_map/all_gather | solution.py:45
  514.8 8.3 %all-gather.13 = f32[4,1,256]{2,1,0:T(1,128)S(1)} all-gather(f32[1,1,256]{2,1,0:T(1,128)S(1)} %bitcast.18), channel_id=7, replica_groups=mesh['row_0'=4,'row_1'=4,'col_0'=4,'col_1'=2] {'row_1'}, dimensions={0}, use_global_device_ids=true | all-gather | bytes 5120 | tf_op jit(solution)/shard_map/all_gather | solution.py:45
  523.2 19.2 %all-gather.14 = f32[4,1,256]{2,1,0:T(1,128)S(1)} all-gather(f32[1,1,256]{2,1,0:T(1,128)S(1)} %bitcast.19), channel_id=8, replica_groups=mesh['row_0'=4,'row_1'=4,'col_0'=4,'col_1'=2] {'col_0'}, dimensions={0}, use_global_device_ids=true | all-gather | bytes 5120 | tf_op jit(solution)/shard_map/all_gather | solution.py:45
  544.2 8.6 %all-gather.8 = f32[4,1,256]{2,1,0:T(1,128)S(1)} all-gather(f32[1,1,256]{2,1,0:T(1,128)S(1)} %bitcast.24), channel_id=2, replica_groups=mesh['row_0'=4,'row_1'=4,'col_0'=4,'col_1'=2] {'row_0'}, dimensions={0}, use_global_device_ids=true | all-gather | bytes 5120 | tf_op jit(solution)/shard_map/all_gather | solution.py:45
  552.9 7.4 %all-gather.9 = f32[4,1,256]{2,1,0:T(1,128)S(1)} all-gather(f32[1,1,256]{2,1,0:T(1,128)S(1)} %bitcast.21), channel_id=3, replica_groups=mesh['row_0'=4,'row_1'=4,'col_0'=4,'col_1'=2] {'row_1'}, dimensions={0}, use_global_device_ids=true | all-gather | bytes 5120 | tf_op jit(solution)/shard_map/all_gather | solution.py:45
  560.3 7.0 all-gather.10
  574.2 6.9 all-to-all-start.6
  581.1 29.0 %all-to-all-done.6 = bf16[16,256,256]{2,1,0:T(8,128)(2,1)} async-done(((bf16[16,256,256]{2,1,0:T(8,128)(2,1)}), bf16[16,256,256]{2,1,0:T(8,128)(2,1)}, u32[]{:S(2)}, u32[]{:S(2)}) %all-to-all-start.6) | async-done | bytes 2097184 | tf_op jit(solution)/shard_map/all_to_all | solution.py:18
  610.2 93.5 %while.47 = (s32[]{:T(128)}, f32[8,256,256]{2,1,0:T(8,128)S(1)}, s32[]{:T(128)}, s32[96]{0:T(128)S(1)}, s32[]{:T(128)}, /*index=5*/bf16[96,256,256]{2,1,0:T(8,12...) while((s32[]{:T(128)}, f32[8,256,256]{2,1,0:T(8,128)S(1)}, ...), condition=%wide.region_24.27_spmd.clone, body=%wide.region_22.26_spmd.clone.sunk | while | flops 540017856 | bytes 25170616 | solution.py:71
  614.8 4.9 convolution_select_fusion.11
  619.8 6.2 scatter_fusion.3
  630.3 4.9 convolution_select_fusion.11
  635.4 6.1 scatter_fusion.3
  645.9 4.9 convolution_select_fusion.11
  650.9 6.2 scatter_fusion.3
  661.5 4.9 convolution_select_fusion.11
  666.5 6.1 scatter_fusion.3
  677.0 4.9 convolution_select_fusion.11
  682.0 6.2 scatter_fusion.3
  692.5 4.9 convolution_select_fusion.11
  697.6 6.1 scatter_fusion.3
  703.7 30.4 %all_to_all.42 = f32[8,256,256]{2,1,0:T(8,128)} all-to-all(f32[8,256,256]{2,1,0:T(8,128)S(1)} %get-tuple-element.199), channel_id=1, replica_groups=mesh['row_0'=4,'row_1'=4,'col_0'=4,'col_1'=2] {'col_0','col_1'}, dimensions={0} | all-to-all | bytes 4194304 | tf_op jit(solution)/shard_map/all_to_all | solution.py:39
  (167 shorter events, 122.4 us)
Async XLA Ops:
  2.7 21.6 %all-to-all-start = ((bf16[8,256,256]{2,1,0:T(8,128)(2,1)}), bf16[8,256,256]{2,1,0:T(8,128)(2,1)S(1)}, u32[]{:S(2)}, u32[]{:S(2)}) async-start(bf16[8,256,256]{2,1,0:T(8,128)(2,1)} %broadcast_in_dim.85), calls=%async_computation | async-start | bytes 2097152 | tf_op jit(solution)/shard_map/all_to_all | solution.py:18
  24.3 2.4 copy-start.12
  24.3 2.4 copy-start.13
  174.5 2.6 copy-start.4
  174.5 2.6 copy-start.6
  174.5 2.6 copy-start.8
  174.5 2.6 copy-start.10
  174.5 2.6 copy-start.14
  177.2 0.7 copy-start
  179.5 32.0 %all-to-all-start.2 = ((bf16[16,256,256]{2,1,0:T(8,128)(2,1)}), bf16[16,256,256]{2,1,0:T(8,128)(2,1)}, u32[]{:S(2)}, u32[]{:S(2)}) async-start(bf16[16,256,256]{2,1,0:T(8,128)(2,1)} %broadcast_in_dim.86), calls=%async_computation.2 | async-start | bytes 4194304 | tf_op jit(solution)/shard_map/all_to_all | solution.py:18
  338.4 1.8 copy-start.2
  338.4 1.8 copy-start.5
  338.4 1.8 copy-start.15
  341.5 19.4 %all-to-all-start.4 = ((bf16[8,256,256]{2,1,0:T(8,128)(2,1)}), bf16[8,256,256]{2,1,0:T(8,128)(2,1)S(1)}, u32[]{:S(2)}, u32[]{:S(2)}) async-start(bf16[8,256,256]{2,1,0:T(8,128)(2,1)} %broadcast_in_dim.87), calls=%async_computation.4 | async-start | bytes 2097152 | tf_op jit(solution)/shard_map/all_to_all | solution.py:18
  455.9 113.3 %all-to-all-start.5 = ((f32[16,256,256]{2,1,0:T(8,128)}), f32[16,256,256]{2,1,0:T(8,128)}, u32[]{:S(2)}, u32[]{:S(2)}) async-start(f32[16,256,256]{2,1,0:T(8,128)} %get-tuple-element.198), calls=%async_computation.5 | async-start | bytes 8388608 | tf_op jit(solution)/shard_map/all_to_all | solution.py:39
  569.2 2.6 copy-start.1
  569.2 2.6 copy-start.7
  569.2 2.6 copy-start.9
  569.2 2.6 copy-start.11
  574.2 35.9 %all-to-all-start.6 = ((bf16[16,256,256]{2,1,0:T(8,128)(2,1)}), bf16[16,256,256]{2,1,0:T(8,128)(2,1)}, u32[]{:S(2)}, u32[]{:S(2)}) async-start(bf16[16,256,256]{2,1,0:T(8,128)(2,1)} %broadcast_in_dim.88), calls=%async_computation.6 | async-start | bytes 4194304 | tf_op jit(solution)/shard_map/all_to_all | solution.py:18
  734.1 1.8 copy-start.3
